TPU v7x, 512 devices: a whole 4x4x16 slice. The times are simulated.
512 devices in a mesh: env: 64 (over x, z), feat: 8 (over y, core).
Axes of the slice: x: 4, y: 4, z: 16, core: 2. Of those that a mesh axis runs over, the one named last changes fastest.
Arguments:
- observations: bfloat16 [32768, 8192], P('env', 'feat'), may hold values from -256 to 256, as said below
- prior_count: int32 [8192], P('feat'), may hold values from 8192 to 131071
- prior_mean: float32 [8192], P('feat'), may hold values from -12 to 12
- prior_var: float32 [8192], P('feat'), may hold values from 0.5 to 40
- policy_weight: bfloat16 [8192, 4096], P('feat', 'env'), may hold values from -0.0625 to 0.0625
Outputs:
- run_mean: float32 [8192], P('feat')
- run_var: float32 [8192], P('feat')
- logits: bfloat16 [32768, 4096], P('env', 'feat')
Inputs may be any that keep to these rules, and one draw needn't show every extreme that they name: observations have per-environment scales and per-feature offsets.
All inputs are finite; a program needn't handle non-finite values.
Results may differ from a plain program's by a relative error of at most 0.013.
Values may be sent and summed in bfloat16 or wider, within the bound.
No kernel may reach another device: no remote copies, remote signals or barrier semaphores. Data moves between devices by JAX's collectives and lax.ppermute only.
A program may use at most 64 MiB of HBM per device.

v0:
```python
import functools

import jax
import jax.numpy as jnp
import numpy as np
from jax import lax
from jax.experimental import pallas as pl
from jax.experimental.pallas import tpu as pltpu
from jax.sharding import Mesh
from jax.sharding import PartitionSpec as P

ENV = ("x", "z")
FEAT = ("y", "c")
SIZES = {"x": 4, "z": 16, "y": 4, "c": 2}
AXES = tuple(SIZES)
SHAPE = tuple(SIZES.values())

BLOCKS = (0, 1, 3, 2)


def fetch(value, source):
    pairs = []
    for to in range(int(np.prod(SHAPE))):
        at = source(*(int(k) for k in np.unravel_index(to, SHAPE)))
        at = tuple(k % n for k, n in zip(at, SHAPE))
        pairs.append((int(np.ravel_multi_index(at, SHAPE)), to))
    return lax.ppermute(value, AXES, pairs)


def along_x(value, by):
    return fetch(value, lambda x, z, y, c: (x + by, z, y, c))


def holder(x, q):
    q = q % 16
    return q % 4, 4 * (q // 4) + x


def across(value):
    return fetch(value, lambda x, z, y, c: (x, z, y, 1 - c))


def along_z(value, by):
    return fetch(value, lambda x, z, y, c: (x, z + (by if c else -by), y, c))


def sum_over(value, axis):
    copies = jnp.broadcast_to(value[None], (lax.axis_size(axis), *value.shape))
    copies = lax.all_to_all(copies, axis, 0, 0)
    return copies.sum(axis=0)


def normal_kernel(mean, factor, *refs):
    for k, block in enumerate(refs[:-1]):
        value = (block[...].astype(jnp.float32) - mean[...]) * factor[...]
        refs[-1][k] = jnp.clip(value, -5.0, 5.0).astype(jnp.bfloat16)


def normal(blocks, mean, factor):
    rows, depth = blocks[0].shape
    tile = rows // 4
    line = pl.BlockSpec((1, depth), lambda k: (0, 0))
    return pl.pallas_call(
        normal_kernel,
        out_shape=jax.ShapeDtypeStruct((4, rows, depth), jnp.bfloat16),
        grid=(rows // tile,),
        in_specs=[line, line] + [pl.BlockSpec((tile, depth), lambda k: (k, 0))] * 4,
        out_specs=pl.BlockSpec((4, tile, depth), lambda k: (0, k, 0)),
        compiler_params=pltpu.CompilerParams(vmem_limit_bytes=12 * 1024 * 1024),
        cost_estimate=pl.CostEstimate(
            flops=20 * rows * depth, bytes_accessed=16 * rows * depth, transcendentals=0
        ),
    )(mean[None], factor[None], *blocks)


def product_kernel(side, order, places, *refs):
    slots, value = refs[:8], refs[8]
    *before, out, weight, held, sem, held_sem = refs[9:]
    step = pl.program_id(0)
    width = slots[0].shape[0] // 2

    def copy(k):
        return pltpu.make_async_copy(
            slots[k].at[pl.ds(side * width, width)],
            weight.at[pl.ds(pl.multiple_of(places[k] * width, width), width)],
            sem.at[k],
        )

    def fetched(k):
        return pltpu.make_async_copy(value.at[k], held.at[k], held_sem.at[k])

    @pl.when(step == 0)
    def _():
        for k in range(8):
            copy(k).start()
        for k in range(4):
            fetched(k).start()
        for k in range(8):
            copy(k).wait()

    fetched(step).wait()
    total = lax.dot_general(
        weight[...], held[step], (((1,), (1,)), ((), ())), preferred_element_type=jnp.float32
    )
    if before:
        total = total + before[0][0].astype(jnp.float32)
    out[0] = total.astype(out.dtype)


def product(side, order, places, slots, value, *before):
    _, rows, depth = value.shape
    columns = 4 * slots[0].shape[0]
    to = (lambda k, order, *_: (order[k], 0, 0)) if before else (lambda k, *_: (k, 0, 0))
    return pl.pallas_call(
        functools.partial(product_kernel, side),
        out_shape=jax.ShapeDtypeStruct((4, columns, rows), jnp.bfloat16),
        grid_spec=pltpu.PrefetchScalarGridSpec(
            num_scalar_prefetch=2,
            grid=(4,),
            in_specs=[pl.BlockSpec(memory_space=pl.ANY)] * 9
            + [pl.BlockSpec((1, columns, rows), lambda k, *_: (k, 0, 0))] * len(before),
            out_specs=pl.BlockSpec((1, columns, rows), to),
            scratch_shapes=[
                pltpu.VMEM((columns, depth), jnp.bfloat16),
                pltpu.VMEM(value.shape, jnp.bfloat16),
                pltpu.SemaphoreType.DMA((8,)),
                pltpu.SemaphoreType.DMA((4,)),
            ],
        ),
        compiler_params=pltpu.CompilerParams(vmem_limit_bytes=16 * 1024 * 1024),
        cost_estimate=pl.CostEstimate(
            flops=8 * columns * rows * depth, bytes_accessed=9 << 20, transcendentals=0
        ),
    )(order, places, *slots, value, *before)


def step(observations, prior_count, prior_mean, prior_var, policy_weight):
    rows, _ = observations.shape
    x, z, y, c = (lax.axis_index(a) for a in AXES)
    batch_n = jnp.float32(rows * lax.axis_size(ENV))

    own = policy_weight.T
    slots = [
        jnp.concatenate(
            [
                fetch(own, lambda x, z, y, c: (*holder(x, z + c), y, c)),
                fetch(own, lambda x, z, y, c: (*holder(x, z + c), y, 1 - c)),
            ],
            axis=0,
        )
    ]
    slots.append(along_z(slots[0], 1))
    for k in range(2, 8):
        slots.append(along_z(slots[k - 2], 2))

    off = observations.astype(jnp.float32) - prior_mean
    sums = jnp.stack([jnp.sum(off, axis=0), jnp.sum(off * off, axis=0)])
    sums = sum_over(sums.reshape(16, 128), "x")
    sums = sum_over(sums, "z").reshape(2, -1)
    count = prior_count.astype(jnp.float32)
    total = count + batch_n
    run_mean = prior_mean + sums[0] / total
    run_var = (prior_var * count + (sums[1] - sums[0] * sums[0] / total)) / total
    scale = 1.0 / jnp.sqrt(run_var + 1e-05)

    blocks = [along_x(observations, by) if by else observations for by in BLOCKS]
    q = jnp.where(c == 0, z - jnp.arange(8), z + 1 + jnp.arange(8)) % 16
    places = (2 * (q % 4) + (q // 4) % 2).astype(jnp.int32)
    order = ((x + jnp.array(BLOCKS)) % 4).astype(jnp.int32)
    value = normal(blocks, run_mean, scale)
    part = product(0, order, places, slots, value)
    value = across(value)
    part = product(1, order, places, slots, value, part)

    part = lax.all_to_all(part.reshape(16, -1, rows), ("x", "y"), 0, 0)
    summed = part.reshape(4, 4, 2, -1, rows).astype(jnp.float32).sum(axis=1)
    summed = summed.astype(jnp.bfloat16)
    other = across(summed)
    sides = []
    for half in range(2):
        q = 4 * (2 * c + half) + y
        mine = jnp.where(c == 0, z - q, q - z - 1) % 16 < 8
        sides.append(jnp.where(mine, summed[:, half], other[:, half]))
    logits = jnp.concatenate(sides, axis=0).reshape(-1, rows).T
    return (run_mean, run_var, logits)


def solution(mesh):
    torus = Mesh(mesh.devices.reshape(SHAPE), AXES)
    in_specs = (P(ENV, FEAT), P(FEAT), P(FEAT), P(FEAT), P(FEAT, ENV))
    out_specs = (P(FEAT), P(FEAT), P(ENV, FEAT))
    return jax.shard_map(step, mesh=torus, in_specs=in_specs, out_specs=out_specs, check_vma=False)
```

profile of v0, /device:TPU:1, one launch (start us, length us, event | category | flops | bytes accessed | tf_op | source)
XLA Modules:
  0.0 211.0 jit_solution(16292864637373587336)
XLA Ops:
  0.6 0.0 copy-start
  0.6 5.3 %collective-permute-start.9 = (bf16[512,1024]{1,0:T(8,128)(2,1)}, bf16[512,1024]{1,0:T(8,128)(2,1)S(1)}, u32[]{:S(2)}, u32[]{:S(2)}) collective-permute-start(bf16[512,1024]{1,0:T(8,128)(2,1)} %refs_0_.1), channel_id=1, source_target_pairs={{128,0},{129,1},{130,2},{131,3},{132,4},{133,5},{134,6},{135,7},{1... | collective-permute-start | bytes 3145736 | tf_op jit(solution)/shard_map/ppermute | solution.py:27
  6.0 1.9 collective-permute-start.10
  7.9 3.6 %collective-permute-start.11 = (bf16[512,1024]{1,0:T(8,128)(2,1)}, bf16[512,1024]{1,0:T(8,128)(2,1)}, u32[]{:S(2)}, u32[]{:S(2)}) collective-permute-start(bf16[512,1024]{1,0:T(8,128)(2,1)} %refs_0_.1), channel_id=1, source_target_pairs={{256,0},{257,1},{258,2},{259,3},{260,4},{261,5},{262,6},{263,7},{2... | collective-permute-start | bytes 3145736 | tf_op jit(solution)/shard_map/ppermute | solution.py:27
  11.5 1.6 fusion
  13.2 41.9 %all_to_all.15 = f32[4,16,128]{2,1,0:T(8,128)S(1)} all-to-all(f32[4,16,128]{2,1,0:T(8,128)S(1)} %broadcast_in_dim.21), channel_id=1, replica_groups=mesh['x'=4,'z'=16,'y'=4,'c'=2] {'x'}, dimensions={0} | all-to-all | bytes 65536 | tf_op jit(solution)/shard_map/all_to_all | solution.py:49
  55.1 26.7 %all_to_all.16 = f32[16,16,128]{2,1,0:T(8,128)S(1)} all-to-all(f32[16,16,128]{2,1,0:T(8,128)S(1)} %broadcast_in_dim.22), channel_id=1, replica_groups=mesh['x'=4,'z'=16,'y'=4,'c'=2] {'z'}, dimensions={0} | all-to-all | bytes 262144 | tf_op jit(solution)/shard_map/all_to_all | solution.py:49
  81.8 1.3 add_rsqrt_fusion
  83.1 0.0 copy-start.1
  83.1 0.0 collective-permute-done.9.refs_1_
  83.1 0.0 collective-permute-done.10.refs_2_
  83.1 0.0 collective-permute-done.11.refs_3_
  83.2 0.0 copy-done
  83.2 0.0 copy-start.2
  83.2 0.0 copy-start.3
  83.2 4.5 %shard_map.85.refs_8_ = bf16[4,512,1024]{2,1,0:T(8,128)(2,1)} custom-call(f32[1,1024]{1,0:T(1,128)S(1)} %bitcast.37, f32[1,1024]{1,0:T(1,128)S(1)} %bitcast.38, bf16[512,1024]{1,0:T(8,128)(2,1)S(1)} %copy-done, bf16[512,1024]{1,0:T(8,128)(2,1)S(1)} %collective-permute-done.9.refs_1_, bf16[512,1024]{1,0:T(8,128)(2,1)S(1)} %collective-permute-done.10.refs_2_, ...), custom_call_target="tpu_custom_call" | custom-call | flops 10485760 | bytes 8388608 | tf_op jit(solution)/shard_map/pallas_call | solution.py:63
  87.7 0.0 copy-done.1
  87.7 6.1 %collective-permute-start.12 = (bf16[4,512,1024]{2,1,0:T(8,128)(2,1)}, bf16[4,512,1024]{2,1,0:T(8,128)(2,1)}, u32[]{:S(2)}, u32[]{:S(2)}) collective-permute-start(bf16[4,512,1024]{2,1,0:T(8,128)(2,1)} %shard_map.85.refs_8_), channel_id=1, source_target_pairs={{1,0},{0,1},{3,2},{2,3},{5,4},{4,5},{7,6},{6,7},{9,8},{8,9},{11,10... | collective-permute-start | bytes 12582920 | tf_op jit(solution)/shard_map/ppermute | solution.py:27
  93.9 0.0 copy-done.2
  93.9 4.0 %collective-permute-start = (bf16[64,1024]{1,0:T(8,128)(2,1)S(1)}, bf16[64,1024]{1,0:T(8,128)(2,1)S(1)}, u32[]{:S(2)}, u32[]{:S(2)}) collective-permute-start(bf16[64,1024]{1,0:T(8,128)(2,1)S(1)} %bitcast.43), channel_id=1, source_target_pairs={{0,0},{129,1},{2,2},{131,3},{4,4},{133,5},{6,6},{135,7},{128,8},{2... | collective-permute-start | bytes 393224 | tf_op jit(solution)/shard_map/ppermute | solution.py:27
  97.9 1.9 collective-permute-start.1
  99.8 0.7 collective-permute-done
  100.6 3.6 %collective-permute-done.1 = bf16[64,1024]{1,0:T(8,128)(2,1)S(1)} collective-permute-done((bf16[64,1024]{1,0:T(8,128)(2,1)S(1)}, bf16[64,1024]{1,0:T(8,128)(2,1)S(1)}, u32[]{:S(2)}, u32[]{:S(2)}) %collective-permute-start.1) | collective-permute-done | bytes 131104 | tf_op jit(solution)/shard_map/ppermute | solution.py:27
  104.2 6.6 %collective-permute-start.2 = (bf16[128,1024]{1,0:T(8,128)(2,1)S(1)}, bf16[128,1024]{1,0:T(8,128)(2,1)S(1)}, u32[]{:S(2)}, u32[]{:S(2)}) collective-permute-start(bf16[128,1024]{1,0:T(8,128)(2,1)S(1)} %constant_dynamic-update-slice_fusion.refs_0_), channel_id=1, source_target_pairs={{120,0},{9,1},{122,2},{11,3},{124,4},{13,5},{126,6},{15,7},{0,8},{... | collective-permute-start | bytes 786440 | tf_op jit(solution)/shard_map/ppermute | solution.py:27
  110.8 8.3 %collective-permute-start.3 = (bf16[128,1024]{1,0:T(8,128)(2,1)S(1)}, bf16[128,1024]{1,0:T(8,128)(2,1)S(1)}, u32[]{:S(2)}, u32[]{:S(2)}) collective-permute-start(bf16[128,1024]{1,0:T(8,128)(2,1)S(1)} %constant_dynamic-update-slice_fusion.refs_0_), channel_id=1, source_target_pairs={{112,0},{17,1},{114,2},{19,3},{116,4},{21,5},{118,6},{23,7},{120,8... | collective-permute-start | bytes 786440 | tf_op jit(solution)/shard_map/ppermute | solution.py:27
  119.1 0.8 collective-permute-done.2.refs_1_
  119.9 2.5 %collective-permute-start.4 = (bf16[128,1024]{1,0:T(8,128)(2,1)S(1)}, bf16[128,1024]{1,0:T(8,128)(2,1)S(1)}, u32[]{:S(2)}, u32[]{:S(2)}) collective-permute-start(bf16[128,1024]{1,0:T(8,128)(2,1)S(1)} %collective-permute-done.2.refs_1_), channel_id=1, source_target_pairs={{112,0},{17,1},{114,2},{19,3},{116,4},{21,5},{118,6},{23,7},{120,8... | collective-permute-start | bytes 786440 | tf_op jit(solution)/shard_map/ppermute | solution.py:27
  122.4 4.7 %collective-permute-done.3.refs_2_ = bf16[128,1024]{1,0:T(8,128)(2,1)S(1)} collective-permute-done((bf16[128,1024]{1,0:T(8,128)(2,1)S(1)}, bf16[128,1024]{1,0:T(8,128)(2,1)S(1)}, u32[]{:S(2)}, u32[]{:S(2)}) %collective-permute-start.3) | collective-permute-done | bytes 262176 | tf_op jit(solution)/shard_map/ppermute | solution.py:27
  127.0 3.8 %collective-permute-start.5 = (bf16[128,1024]{1,0:T(8,128)(2,1)S(1)}, bf16[128,1024]{1,0:T(8,128)(2,1)S(1)}, u32[]{:S(2)}, u32[]{:S(2)}) collective-permute-start(bf16[128,1024]{1,0:T(8,128)(2,1)S(1)} %collective-permute-done.3.refs_2_), channel_id=1, source_target_pairs={{112,0},{17,1},{114,2},{19,3},{116,4},{21,5},{118,6},{23,7},{120,8... | collective-permute-start | bytes 786440 | tf_op jit(solution)/shard_map/ppermute | solution.py:27
  130.8 0.5 collective-permute-done.4.refs_3_
  131.3 2.6 %collective-permute-start.6 = (bf16[128,1024]{1,0:T(8,128)(2,1)S(1)}, bf16[128,1024]{1,0:T(8,128)(2,1)S(1)}, u32[]{:S(2)}, u32[]{:S(2)}) collective-permute-start(bf16[128,1024]{1,0:T(8,128)(2,1)S(1)} %collective-permute-done.4.refs_3_), channel_id=1, source_target_pairs={{112,0},{17,1},{114,2},{19,3},{116,4},{21,5},{118,6},{23,7},{120,8... | collective-permute-start | bytes 786440 | tf_op jit(solution)/shard_map/ppermute | solution.py:27
  133.9 4.4 %collective-permute-done.5.refs_4_ = bf16[128,1024]{1,0:T(8,128)(2,1)S(1)} collective-permute-done((bf16[128,1024]{1,0:T(8,128)(2,1)S(1)}, bf16[128,1024]{1,0:T(8,128)(2,1)S(1)}, u32[]{:S(2)}, u32[]{:S(2)}) %collective-permute-start.5) | collective-permute-done | bytes 262176 | tf_op jit(solution)/shard_map/ppermute | solution.py:27
  138.3 4.9 %collective-permute-start.7 = (bf16[128,1024]{1,0:T(8,128)(2,1)S(1)}, bf16[128,1024]{1,0:T(8,128)(2,1)S(1)}, u32[]{:S(2)}, u32[]{:S(2)}) collective-permute-start(bf16[128,1024]{1,0:T(8,128)(2,1)S(1)} %collective-permute-done.5.refs_4_), channel_id=1, source_target_pairs={{112,0},{17,1},{114,2},{19,3},{116,4},{21,5},{118,6},{23,7},{120,8... | collective-permute-start | bytes 786440 | tf_op jit(solution)/shard_map/ppermute | solution.py:27
  143.2 0.0 collective-permute-done.6.refs_5_
  143.2 3.0 %collective-permute-start.8 = (bf16[128,1024]{1,0:T(8,128)(2,1)S(1)}, bf16[128,1024]{1,0:T(8,128)(2,1)S(1)}, u32[]{:S(2)}, u32[]{:S(2)}) collective-permute-start(bf16[128,1024]{1,0:T(8,128)(2,1)S(1)} %collective-permute-done.6.refs_5_), channel_id=1, source_target_pairs={{112,0},{17,1},{114,2},{19,3},{116,4},{21,5},{118,6},{23,7},{120,8... | collective-permute-start | bytes 786440 | tf_op jit(solution)/shard_map/ppermute | solution.py:27
  146.3 0.0 copy-done.3
  146.3 3.9 %collective-permute-done.7.refs_6_ = bf16[128,1024]{1,0:T(8,128)(2,1)S(1)} collective-permute-done((bf16[128,1024]{1,0:T(8,128)(2,1)S(1)}, bf16[128,1024]{1,0:T(8,128)(2,1)S(1)}, u32[]{:S(2)}, u32[]{:S(2)}) %collective-permute-start.7) | collective-permute-done | bytes 262176 | tf_op jit(solution)/shard_map/ppermute | solution.py:27
  150.2 2.7 %collective-permute-done.8.refs_7_ = bf16[128,1024]{1,0:T(8,128)(2,1)S(1)} collective-permute-done((bf16[128,1024]{1,0:T(8,128)(2,1)S(1)}, bf16[128,1024]{1,0:T(8,128)(2,1)S(1)}, u32[]{:S(2)}, u32[]{:S(2)}) %collective-permute-start.8) | collective-permute-done | bytes 262176 | tf_op jit(solution)/shard_map/ppermute | solution.py:27
  152.9 6.3 %shard_map.86.refs_9_ = bf16[4,512,512]{2,1,0:T(8,128)(2,1)S(1)} custom-call(s32[4]{0:T(128)S(1)} %and_select_fusion.4.order, s32[8]{0:T(128)S(1)} %fusion.7.places, bf16[128,1024]{1,0:T(8,128)(2,1)S(1)} %constant_dynamic-update-slice_fusion.refs_0_, bf16[128,1024]{1,0:T(8,128)(2,1)S(1)} %collective-permute-done.2.refs_1_, ...), custom_call_target="tpu_custom_call" | custom-call | flops 2147483648 | bytes 9437184 | tf_op jit(solution)/shard_map/pallas_call | solution.py:114
  159.2 0.0 collective-permute-done.12.refs_8_
  159.2 6.3 %shard_map.87 = bf16[4,512,512]{2,1,0:T(8,128)(2,1)S(1)} custom-call(s32[4]{0:T(128)S(1)} %and_select_fusion.4.order, s32[8]{0:T(128)S(1)} %fusion.7.places, bf16[128,1024]{1,0:T(8,128)(2,1)S(1)} %constant_dynamic-update-slice_fusion.refs_0_, bf16[128,1024]{1,0:T(8,128)(2,1)S(1)} %collective-permute-done.2.refs_1_, ...), custom_call_target="tpu_custom_call" | custom-call | flops 2147483648 | bytes 9437184 | tf_op jit(solution)/shard_map/pallas_call | solution.py:114
  165.6 35.5 %all_to_all.17 = bf16[16,128,512]{2,1,0:T(8,128)(2,1)S(1)} all-to-all(bf16[16,128,512]{2,1,0:T(8,128)(2,1)S(1)} %bitcast.36), channel_id=1, replica_groups=mesh['x'=4,'z'=16,'y'=4,'c'=2] {'x','y'}, dimensions={0} | all-to-all | bytes 4194304 | tf_op jit(solution)/shard_map/all_to_all | solution.py:175
  201.1 0.5 reduce_sum.52
  201.6 6.7 %collective-permute-start.13 = (bf16[4,2,64,512]{3,2,0,1:T(8,128)(2,1)S(1)}, bf16[4,2,64,512]{3,2,0,1:T(8,128)(2,1)S(1)}, u32[]{:S(2)}, u32[]{:S(2)}) collective-permute-start(bf16[4,2,64,512]{3,2,0,1:T(8,128)(2,1)S(1)} %copy.14), channel_id=1, source_target_pairs={{1,0},{0,1},{3,2},{2,3},{5,4},{4,5},{7,6},{6,7},{9,8},{8,9},{11,10... | collective-permute-start | bytes 1572872 | tf_op jit(solution)/shard_map/ppermute | solution.py:27
  208.4 1.5 collective-permute-done.13
  209.9 0.1 fusion.3
  210.0 1.0 copy.17
  (13 shorter events, 0.2 us)
Async XLA Ops:
  0.6 82.5 %copy-start = (bf16[512,1024]{1,0:T(8,128)(2,1)S(1)}, bf16[512,1024]{1,0:T(8,128)(2,1)}, u32[]{:S(2)}) copy-start(bf16[512,1024]{1,0:T(8,128)(2,1)} %refs_0_.1) | copy-start | bytes 3145732
  0.6 82.5 %collective-permute-start.9 = (bf16[512,1024]{1,0:T(8,128)(2,1)}, bf16[512,1024]{1,0:T(8,128)(2,1)S(1)}, u32[]{:S(2)}, u32[]{:S(2)}) collective-permute-start(bf16[512,1024]{1,0:T(8,128)(2,1)} %refs_0_.1), channel_id=1, source_target_pairs={{128,0},{129,1},{130,2},{131,3},{132,4},{133,5},{134,6},{135,7},{1... | collective-permute-start | bytes 3145736 | tf_op jit(solution)/shard_map/ppermute | solution.py:27
  6.0 77.2 %collective-permute-start.10 = (bf16[512,1024]{1,0:T(8,128)(2,1)}, bf16[512,1024]{1,0:T(8,128)(2,1)S(1)}, u32[]{:S(2)}, u32[]{:S(2)}) collective-permute-start(bf16[512,1024]{1,0:T(8,128)(2,1)} %refs_0_.1), channel_id=1, source_target_pairs={{384,0},{385,1},{386,2},{387,3},{388,4},{389,5},{390,6},{391,7},{3... | collective-permute-start | bytes 3145736 | tf_op jit(solution)/shard_map/ppermute | solution.py:27
  7.9 75.2 %collective-permute-start.11 = (bf16[512,1024]{1,0:T(8,128)(2,1)}, bf16[512,1024]{1,0:T(8,128)(2,1)}, u32[]{:S(2)}, u32[]{:S(2)}) collective-permute-start(bf16[512,1024]{1,0:T(8,128)(2,1)} %refs_0_.1), channel_id=1, source_target_pairs={{256,0},{257,1},{258,2},{259,3},{260,4},{261,5},{262,6},{263,7},{2... | collective-permute-start | bytes 3145736 | tf_op jit(solution)/shard_map/ppermute | solution.py:27
  83.1 4.6 %copy-start.1 = (f32[1024]{0:T(1024)}, f32[1024]{0:T(1024)S(1)}, u32[]{:S(2)}) copy-start(f32[1024]{0:T(1024)S(1)} %get-tuple-element.16) | copy-start | bytes 12292
  83.2 10.7 %copy-start.2 = (bf16[1024,64]{0,1:T(8,128)(2,1)S(1)}, bf16[1024,64]{0,1:T(8,128)(2,1)}, u32[]{:S(2)}) copy-start(bf16[1024,64]{0,1:T(8,128)(2,1)} %param.10) | copy-start | bytes 393220
  83.2 63.1 %copy-start.3 = (s32[4]{0:T(128)S(1)}, s32[4]{0:T(128)}, u32[]{:S(2)}) copy-start(s32[4]{0:T(128)} %constant.102.clone) | copy-start | bytes 52
  87.7 71.5 %collective-permute-start.12 = (bf16[4,512,1024]{2,1,0:T(8,128)(2,1)}, bf16[4,512,1024]{2,1,0:T(8,128)(2,1)}, u32[]{:S(2)}, u32[]{:S(2)}) collective-permute-start(bf16[4,512,1024]{2,1,0:T(8,128)(2,1)} %shard_map.85.refs_8_), channel_id=1, source_target_pairs={{1,0},{0,1},{3,2},{2,3},{5,4},{4,5},{7,6},{6,7},{9,8},{8,9},{11,10... | collective-permute-start | bytes 12582920 | tf_op jit(solution)/shard_map/ppermute | solution.py:27
  93.9 6.7 %collective-permute-start = (bf16[64,1024]{1,0:T(8,128)(2,1)S(1)}, bf16[64,1024]{1,0:T(8,128)(2,1)S(1)}, u32[]{:S(2)}, u32[]{:S(2)}) collective-permute-start(bf16[64,1024]{1,0:T(8,128)(2,1)S(1)} %bitcast.43), channel_id=1, source_target_pairs={{0,0},{129,1},{2,2},{131,3},{4,4},{133,5},{6,6},{135,7},{128,8},{2... | collective-permute-start | bytes 393224 | tf_op jit(solution)/shard_map/ppermute | solution.py:27
  97.9 6.3 %collective-permute-start.1 = (bf16[64,1024]{1,0:T(8,128)(2,1)S(1)}, bf16[64,1024]{1,0:T(8,128)(2,1)S(1)}, u32[]{:S(2)}, u32[]{:S(2)}) collective-permute-start(bf16[64,1024]{1,0:T(8,128)(2,1)S(1)} %bitcast.44), channel_id=1, source_target_pairs={{1,0},{128,1},{3,2},{130,3},{5,4},{132,5},{7,6},{134,7},{129,8},{2... | collective-permute-start | bytes 393224 | tf_op jit(solution)/shard_map/ppermute | solution.py:27
  104.2 15.7 %collective-permute-start.2 = (bf16[128,1024]{1,0:T(8,128)(2,1)S(1)}, bf16[128,1024]{1,0:T(8,128)(2,1)S(1)}, u32[]{:S(2)}, u32[]{:S(2)}) collective-permute-start(bf16[128,1024]{1,0:T(8,128)(2,1)S(1)} %constant_dynamic-update-slice_fusion.refs_0_), channel_id=1, source_target_pairs={{120,0},{9,1},{122,2},{11,3},{124,4},{13,5},{126,6},{15,7},{0,8},{... | collective-permute-start | bytes 786440 | tf_op jit(solution)/shard_map/ppermute | solution.py:27
  110.8 16.3 %collective-permute-start.3 = (bf16[128,1024]{1,0:T(8,128)(2,1)S(1)}, bf16[128,1024]{1,0:T(8,128)(2,1)S(1)}, u32[]{:S(2)}, u32[]{:S(2)}) collective-permute-start(bf16[128,1024]{1,0:T(8,128)(2,1)S(1)} %constant_dynamic-update-slice_fusion.refs_0_), channel_id=1, source_target_pairs={{112,0},{17,1},{114,2},{19,3},{116,4},{21,5},{118,6},{23,7},{120,8... | collective-permute-start | bytes 786440 | tf_op jit(solution)/shard_map/ppermute | solution.py:27
  119.9 11.4 %collective-permute-start.4 = (bf16[128,1024]{1,0:T(8,128)(2,1)S(1)}, bf16[128,1024]{1,0:T(8,128)(2,1)S(1)}, u32[]{:S(2)}, u32[]{:S(2)}) collective-permute-start(bf16[128,1024]{1,0:T(8,128)(2,1)S(1)} %collective-permute-done.2.refs_1_), channel_id=1, source_target_pairs={{112,0},{17,1},{114,2},{19,3},{116,4},{21,5},{118,6},{23,7},{120,8... | collective-permute-start | bytes 786440 | tf_op jit(solution)/shard_map/ppermute | solution.py:27
  127.0 11.3 %collective-permute-start.5 = (bf16[128,1024]{1,0:T(8,128)(2,1)S(1)}, bf16[128,1024]{1,0:T(8,128)(2,1)S(1)}, u32[]{:S(2)}, u32[]{:S(2)}) collective-permute-start(bf16[128,1024]{1,0:T(8,128)(2,1)S(1)} %collective-permute-done.3.refs_2_), channel_id=1, source_target_pairs={{112,0},{17,1},{114,2},{19,3},{116,4},{21,5},{118,6},{23,7},{120,8... | collective-permute-start | bytes 786440 | tf_op jit(solution)/shard_map/ppermute | solution.py:27
  131.3 11.9 %collective-permute-start.6 = (bf16[128,1024]{1,0:T(8,128)(2,1)S(1)}, bf16[128,1024]{1,0:T(8,128)(2,1)S(1)}, u32[]{:S(2)}, u32[]{:S(2)}) collective-permute-start(bf16[128,1024]{1,0:T(8,128)(2,1)S(1)} %collective-permute-done.4.refs_3_), channel_id=1, source_target_pairs={{112,0},{17,1},{114,2},{19,3},{116,4},{21,5},{118,6},{23,7},{120,8... | collective-permute-start | bytes 786440 | tf_op jit(solution)/shard_map/ppermute | solution.py:27
  138.3 11.9 %collective-permute-start.7 = (bf16[128,1024]{1,0:T(8,128)(2,1)S(1)}, bf16[128,1024]{1,0:T(8,128)(2,1)S(1)}, u32[]{:S(2)}, u32[]{:S(2)}) collective-permute-start(bf16[128,1024]{1,0:T(8,128)(2,1)S(1)} %collective-permute-done.5.refs_4_), channel_id=1, source_target_pairs={{112,0},{17,1},{114,2},{19,3},{116,4},{21,5},{118,6},{23,7},{120,8... | collective-permute-start | bytes 786440 | tf_op jit(solution)/shard_map/ppermute | solution.py:27
  143.2 9.7 %collective-permute-start.8 = (bf16[128,1024]{1,0:T(8,128)(2,1)S(1)}, bf16[128,1024]{1,0:T(8,128)(2,1)S(1)}, u32[]{:S(2)}, u32[]{:S(2)}) collective-permute-start(bf16[128,1024]{1,0:T(8,128)(2,1)S(1)} %collective-permute-done.6.refs_5_), channel_id=1, source_target_pairs={{112,0},{17,1},{114,2},{19,3},{116,4},{21,5},{118,6},{23,7},{120,8... | collective-permute-start | bytes 786440 | tf_op jit(solution)/shard_map/ppermute | solution.py:27
  201.6 8.2 %collective-permute-start.13 = (bf16[4,2,64,512]{3,2,0,1:T(8,128)(2,1)S(1)}, bf16[4,2,64,512]{3,2,0,1:T(8,128)(2,1)S(1)}, u32[]{:S(2)}, u32[]{:S(2)}) collective-permute-start(bf16[4,2,64,512]{3,2,0,1:T(8,128)(2,1)S(1)} %copy.14), channel_id=1, source_target_pairs={{1,0},{0,1},{3,2},{2,3},{5,4},{4,5},{7,6},{6,7},{9,8},{8,9},{11,10... | collective-permute-start | bytes 1572872 | tf_op jit(solution)/shard_map/ppermute | solution.py:27
where the time goes:
time: 212 us; the launch traced here: 211 us
  blocking collectives  104 us (49%)
  starting transfers between devices  61.2 us (29%)
  waiting for transfers between devices  22.8 us (11%)
  Pallas kernels  17.1 us (8%)
  other arithmetic  3.63 us (2%)
    all_to_all x2, blocking collectives, sum_over(): copies = lax.all_to_all(copies, axis, 0, 0)  68.6 us
    ppermute x14, starting transfers between devices, fetch(): return lax.ppermute(value, AXES, pairs)  61.2 us
    all_to_all x1, blocking collectives, step(): part = lax.all_to_all(part.reshape(16, -1, rows), ('x', 'y'), 0, 0)  35.5 us
    ppermute x14, waiting for transfers between devices, fetch(): return lax.ppermute(value, AXES, pairs)  22.8 us
    pallas_call x2, Pallas kernels, product(): pl.pallas_call(functools.partial(product_kernel, side), out_shape=jax.Sha...  12.6 us
    pallas_call x1, Pallas kernels, normal(): pl.pallas_call(normal_kernel, out_shape=jax.ShapeDtypeStruct((4, rows, de...  4.55 us
  transfers between devices with their start and end apart: 14, of which 9 were waited for; matrix products, arithmetic and copies ran while one was open for 1% of the time, Pallas kernels for 3%

commit v1 on v0

--- a/solution.py
+++ b/solution.py
@@ -58,7 +58,7 @@
 
 def normal(blocks, mean, factor):
     rows, depth = blocks[0].shape
-    tile = rows // 4
+    tile = rows // 2
     line = pl.BlockSpec((1, depth), lambda k: (0, 0))
     return pl.pallas_call(
         normal_kernel,
@@ -66,7 +66,7 @@
         grid=(rows // tile,),
         in_specs=[line, line] + [pl.BlockSpec((tile, depth), lambda k: (k, 0))] * 4,
         out_specs=pl.BlockSpec((4, tile, depth), lambda k: (0, k, 0)),
-        compiler_params=pltpu.CompilerParams(vmem_limit_bytes=12 * 1024 * 1024),
+        compiler_params=pltpu.CompilerParams(vmem_limit_bytes=24 * 1024 * 1024),
         cost_estimate=pl.CostEstimate(
             flops=20 * rows * depth, bytes_accessed=16 * rows * depth, transcendentals=0
         ),
@@ -98,28 +98,31 @@
         for k in range(8):
             copy(k).wait()
 
-    fetched(step).wait()
-    total = lax.dot_general(
-        weight[...], held[step], (((1,), (1,)), ((), ())), preferred_element_type=jnp.float32
-    )
-    if before:
-        total = total + before[0][0].astype(jnp.float32)
-    out[0] = total.astype(out.dtype)
+    for at in range(out.shape[0]):
+        k = step * out.shape[0] + at
+        fetched(k).wait()
+        total = lax.dot_general(
+            weight[...], held[k], (((1,), (1,)), ((), ())), preferred_element_type=jnp.float32
+        )
+        if before:
+            total = total + before[0][0].astype(jnp.float32)
+        out[at] = total.astype(out.dtype)
 
 
 def product(side, order, places, slots, value, *before):
     _, rows, depth = value.shape
     columns = 4 * slots[0].shape[0]
+    each = 1 if before else 2
     to = (lambda k, order, *_: (order[k], 0, 0)) if before else (lambda k, *_: (k, 0, 0))
     return pl.pallas_call(
         functools.partial(product_kernel, side),
         out_shape=jax.ShapeDtypeStruct((4, columns, rows), jnp.bfloat16),
         grid_spec=pltpu.PrefetchScalarGridSpec(
             num_scalar_prefetch=2,
-            grid=(4,),
+            grid=(4 // each,),
             in_specs=[pl.BlockSpec(memory_space=pl.ANY)] * 9
             + [pl.BlockSpec((1, columns, rows), lambda k, *_: (k, 0, 0))] * len(before),
-            out_specs=pl.BlockSpec((1, columns, rows), to),
+            out_specs=pl.BlockSpec((each, columns, rows), to),
             scratch_shapes=[
                 pltpu.VMEM((columns, depth), jnp.bfloat16),
                 pltpu.VMEM(value.shape, jnp.bfloat16),

time: 212 us -> 211 us (level)
  no operation moved by 1% of the time
where the time goes in v1:
time: 211 us; the launch traced here: 210 us
  blocking collectives  104 us (49%)
  starting transfers between devices  61.2 us (29%)
  waiting for transfers between devices  22.8 us (11%)
  Pallas kernels  16.2 us (8%)
  other arithmetic  3.63 us (2%)
    all_to_all x2, blocking collectives, sum_over(): copies = lax.all_to_all(copies, axis, 0, 0)  68.6 us
    ppermute x14, starting transfers between devices, fetch(): return lax.ppermute(value, AXES, pairs)  61.2 us
    all_to_all x1, blocking collectives, step(): part = lax.all_to_all(part.reshape(16, -1, rows), ('x', 'y'), 0, 0)  35.5 us
    ppermute x14, waiting for transfers between devices, fetch(): return lax.ppermute(value, AXES, pairs)  22.8 us
    pallas_call x2, Pallas kernels, product(): pl.pallas_call(functools.partial(product_kernel, side), out_shape=jax.Sha...  12.6 us
  transfers between devices with their start and end apart: 14, of which 9 were waited for; matrix products, arithmetic and copies ran while one was open for 1% of the time, Pallas kernels for 3%

profile of v1, /device:TPU:1, one launch (start us, length us, event | category | flops | bytes accessed | tf_op | source)
XLA Modules:
  0.0 210.1 jit_solution(16623728487625279398)
XLA Ops:
  0.6 0.0 copy-start
  0.6 5.3 %collective-permute-start.9 = (bf16[512,1024]{1,0:T(8,128)(2,1)}, bf16[512,1024]{1,0:T(8,128)(2,1)S(1)}, u32[]{:S(2)}, u32[]{:S(2)}) collective-permute-start(bf16[512,1024]{1,0:T(8,128)(2,1)} %refs_0_.1), channel_id=1, source_target_pairs={{128,0},{129,1},{130,2},{131,3},{132,4},{133,5},{134,6},{135,7},{1... | collective-permute-start | bytes 3145736 | tf_op jit(solution)/shard_map/ppermute | solution.py:27
  6.0 1.9 collective-permute-start.10
  7.9 3.6 %collective-permute-start.11 = (bf16[512,1024]{1,0:T(8,128)(2,1)}, bf16[512,1024]{1,0:T(8,128)(2,1)}, u32[]{:S(2)}, u32[]{:S(2)}) collective-permute-start(bf16[512,1024]{1,0:T(8,128)(2,1)} %refs_0_.1), channel_id=1, source_target_pairs={{256,0},{257,1},{258,2},{259,3},{260,4},{261,5},{262,6},{263,7},{2... | collective-permute-start | bytes 3145736 | tf_op jit(solution)/shard_map/ppermute | solution.py:27
  11.5 1.6 fusion
  13.2 41.9 %all_to_all.15 = f32[4,16,128]{2,1,0:T(8,128)S(1)} all-to-all(f32[4,16,128]{2,1,0:T(8,128)S(1)} %broadcast_in_dim.21), channel_id=1, replica_groups=mesh['x'=4,'z'=16,'y'=4,'c'=2] {'x'}, dimensions={0} | all-to-all | bytes 65536 | tf_op jit(solution)/shard_map/all_to_all | solution.py:49
  55.1 26.7 %all_to_all.16 = f32[16,16,128]{2,1,0:T(8,128)S(1)} all-to-all(f32[16,16,128]{2,1,0:T(8,128)S(1)} %broadcast_in_dim.22), channel_id=1, replica_groups=mesh['x'=4,'z'=16,'y'=4,'c'=2] {'z'}, dimensions={0} | all-to-all | bytes 262144 | tf_op jit(solution)/shard_map/all_to_all | solution.py:49
  81.8 1.3 add_rsqrt_fusion
  83.1 0.0 copy-start.1
  83.1 0.0 collective-permute-done.9.refs_1_
  83.1 0.0 collective-permute-done.10.refs_2_
  83.1 0.0 collective-permute-done.11.refs_3_
  83.2 0.0 copy-done
  83.2 0.0 copy-start.2
  83.2 0.0 copy-start.3
  83.2 3.7 %shard_map.85.refs_8_ = bf16[4,512,1024]{2,1,0:T(8,128)(2,1)} custom-call(f32[1,1024]{1,0:T(1,128)S(1)} %bitcast.37, f32[1,1024]{1,0:T(1,128)S(1)} %bitcast.38, bf16[512,1024]{1,0:T(8,128)(2,1)S(1)} %copy-done, bf16[512,1024]{1,0:T(8,128)(2,1)S(1)} %collective-permute-done.9.refs_1_, bf16[512,1024]{1,0:T(8,128)(2,1)S(1)} %collective-permute-done.10.refs_2_, ...), custom_call_target="tpu_custom_call" | custom-call | flops 10485760 | bytes 8388608 | tf_op jit(solution)/shard_map/pallas_call | solution.py:63
  86.8 0.0 copy-done.1
  86.8 6.1 %collective-permute-start.12 = (bf16[4,512,1024]{2,1,0:T(8,128)(2,1)}, bf16[4,512,1024]{2,1,0:T(8,128)(2,1)}, u32[]{:S(2)}, u32[]{:S(2)}) collective-permute-start(bf16[4,512,1024]{2,1,0:T(8,128)(2,1)} %shard_map.85.refs_8_), channel_id=1, source_target_pairs={{1,0},{0,1},{3,2},{2,3},{5,4},{4,5},{7,6},{6,7},{9,8},{8,9},{11,10... | collective-permute-start | bytes 12582920 | tf_op jit(solution)/shard_map/ppermute | solution.py:27
  93.0 0.0 copy-done.2
  93.0 4.0 %collective-permute-start = (bf16[64,1024]{1,0:T(8,128)(2,1)S(1)}, bf16[64,1024]{1,0:T(8,128)(2,1)S(1)}, u32[]{:S(2)}, u32[]{:S(2)}) collective-permute-start(bf16[64,1024]{1,0:T(8,128)(2,1)S(1)} %bitcast.43), channel_id=1, source_target_pairs={{0,0},{129,1},{2,2},{131,3},{4,4},{133,5},{6,6},{135,7},{128,8},{2... | collective-permute-start | bytes 393224 | tf_op jit(solution)/shard_map/ppermute | solution.py:27
  97.0 1.9 collective-permute-start.1
  98.9 0.7 collective-permute-done
  99.7 3.6 %collective-permute-done.1 = bf16[64,1024]{1,0:T(8,128)(2,1)S(1)} collective-permute-done((bf16[64,1024]{1,0:T(8,128)(2,1)S(1)}, bf16[64,1024]{1,0:T(8,128)(2,1)S(1)}, u32[]{:S(2)}, u32[]{:S(2)}) %collective-permute-start.1) | collective-permute-done | bytes 131104 | tf_op jit(solution)/shard_map/ppermute | solution.py:27
  103.3 6.6 %collective-permute-start.2 = (bf16[128,1024]{1,0:T(8,128)(2,1)S(1)}, bf16[128,1024]{1,0:T(8,128)(2,1)S(1)}, u32[]{:S(2)}, u32[]{:S(2)}) collective-permute-start(bf16[128,1024]{1,0:T(8,128)(2,1)S(1)} %constant_dynamic-update-slice_fusion.refs_0_), channel_id=1, source_target_pairs={{120,0},{9,1},{122,2},{11,3},{124,4},{13,5},{126,6},{15,7},{0,8},{... | collective-permute-start | bytes 786440 | tf_op jit(solution)/shard_map/ppermute | solution.py:27
  109.9 8.3 %collective-permute-start.3 = (bf16[128,1024]{1,0:T(8,128)(2,1)S(1)}, bf16[128,1024]{1,0:T(8,128)(2,1)S(1)}, u32[]{:S(2)}, u32[]{:S(2)}) collective-permute-start(bf16[128,1024]{1,0:T(8,128)(2,1)S(1)} %constant_dynamic-update-slice_fusion.refs_0_), channel_id=1, source_target_pairs={{112,0},{17,1},{114,2},{19,3},{116,4},{21,5},{118,6},{23,7},{120,8... | collective-permute-start | bytes 786440 | tf_op jit(solution)/shard_map/ppermute | solution.py:27
  118.2 0.8 collective-permute-done.2.refs_1_
  119.0 2.5 %collective-permute-start.4 = (bf16[128,1024]{1,0:T(8,128)(2,1)S(1)}, bf16[128,1024]{1,0:T(8,128)(2,1)S(1)}, u32[]{:S(2)}, u32[]{:S(2)}) collective-permute-start(bf16[128,1024]{1,0:T(8,128)(2,1)S(1)} %collective-permute-done.2.refs_1_), channel_id=1, source_target_pairs={{112,0},{17,1},{114,2},{19,3},{116,4},{21,5},{118,6},{23,7},{120,8... | collective-permute-start | bytes 786440 | tf_op jit(solution)/shard_map/ppermute | solution.py:27
  121.5 4.7 %collective-permute-done.3.refs_2_ = bf16[128,1024]{1,0:T(8,128)(2,1)S(1)} collective-permute-done((bf16[128,1024]{1,0:T(8,128)(2,1)S(1)}, bf16[128,1024]{1,0:T(8,128)(2,1)S(1)}, u32[]{:S(2)}, u32[]{:S(2)}) %collective-permute-start.3) | collective-permute-done | bytes 262176 | tf_op jit(solution)/shard_map/ppermute | solution.py:27
  126.1 3.8 %collective-permute-start.5 = (bf16[128,1024]{1,0:T(8,128)(2,1)S(1)}, bf16[128,1024]{1,0:T(8,128)(2,1)S(1)}, u32[]{:S(2)}, u32[]{:S(2)}) collective-permute-start(bf16[128,1024]{1,0:T(8,128)(2,1)S(1)} %collective-permute-done.3.refs_2_), channel_id=1, source_target_pairs={{112,0},{17,1},{114,2},{19,3},{116,4},{21,5},{118,6},{23,7},{120,8... | collective-permute-start | bytes 786440 | tf_op jit(solution)/shard_map/ppermute | solution.py:27
  129.9 0.5 collective-permute-done.4.refs_3_
  130.4 2.6 %collective-permute-start.6 = (bf16[128,1024]{1,0:T(8,128)(2,1)S(1)}, bf16[128,1024]{1,0:T(8,128)(2,1)S(1)}, u32[]{:S(2)}, u32[]{:S(2)}) collective-permute-start(bf16[128,1024]{1,0:T(8,128)(2,1)S(1)} %collective-permute-done.4.refs_3_), channel_id=1, source_target_pairs={{112,0},{17,1},{114,2},{19,3},{116,4},{21,5},{118,6},{23,7},{120,8... | collective-permute-start | bytes 786440 | tf_op jit(solution)/shard_map/ppermute | solution.py:27
  133.0 4.4 %collective-permute-done.5.refs_4_ = bf16[128,1024]{1,0:T(8,128)(2,1)S(1)} collective-permute-done((bf16[128,1024]{1,0:T(8,128)(2,1)S(1)}, bf16[128,1024]{1,0:T(8,128)(2,1)S(1)}, u32[]{:S(2)}, u32[]{:S(2)}) %collective-permute-start.5) | collective-permute-done | bytes 262176 | tf_op jit(solution)/shard_map/ppermute | solution.py:27
  137.4 4.9 %collective-permute-start.7 = (bf16[128,1024]{1,0:T(8,128)(2,1)S(1)}, bf16[128,1024]{1,0:T(8,128)(2,1)S(1)}, u32[]{:S(2)}, u32[]{:S(2)}) collective-permute-start(bf16[128,1024]{1,0:T(8,128)(2,1)S(1)} %collective-permute-done.5.refs_4_), channel_id=1, source_target_pairs={{112,0},{17,1},{114,2},{19,3},{116,4},{21,5},{118,6},{23,7},{120,8... | collective-permute-start | bytes 786440 | tf_op jit(solution)/shard_map/ppermute | solution.py:27
  142.3 0.0 collective-permute-done.6.refs_5_
  142.3 3.0 %collective-permute-start.8 = (bf16[128,1024]{1,0:T(8,128)(2,1)S(1)}, bf16[128,1024]{1,0:T(8,128)(2,1)S(1)}, u32[]{:S(2)}, u32[]{:S(2)}) collective-permute-start(bf16[128,1024]{1,0:T(8,128)(2,1)S(1)} %collective-permute-done.6.refs_5_), channel_id=1, source_target_pairs={{112,0},{17,1},{114,2},{19,3},{116,4},{21,5},{118,6},{23,7},{120,8... | collective-permute-start | bytes 786440 | tf_op jit(solution)/shard_map/ppermute | solution.py:27
  145.4 0.0 copy-done.3
  145.4 3.9 %collective-permute-done.7.refs_6_ = bf16[128,1024]{1,0:T(8,128)(2,1)S(1)} collective-permute-done((bf16[128,1024]{1,0:T(8,128)(2,1)S(1)}, bf16[128,1024]{1,0:T(8,128)(2,1)S(1)}, u32[]{:S(2)}, u32[]{:S(2)}) %collective-permute-start.7) | collective-permute-done | bytes 262176 | tf_op jit(solution)/shard_map/ppermute | solution.py:27
  149.3 2.7 %collective-permute-done.8.refs_7_ = bf16[128,1024]{1,0:T(8,128)(2,1)S(1)} collective-permute-done((bf16[128,1024]{1,0:T(8,128)(2,1)S(1)}, bf16[128,1024]{1,0:T(8,128)(2,1)S(1)}, u32[]{:S(2)}, u32[]{:S(2)}) %collective-permute-start.8) | collective-permute-done | bytes 262176 | tf_op jit(solution)/shard_map/ppermute | solution.py:27
  152.0 6.3 %shard_map.86.refs_9_ = bf16[4,512,512]{2,1,0:T(8,128)(2,1)S(1)} custom-call(s32[4]{0:T(128)S(1)} %and_select_fusion.4.order, s32[8]{0:T(128)S(1)} %fusion.7.places, bf16[128,1024]{1,0:T(8,128)(2,1)S(1)} %constant_dynamic-update-slice_fusion.refs_0_, bf16[128,1024]{1,0:T(8,128)(2,1)S(1)} %collective-permute-done.2.refs_1_, ...), custom_call_target="tpu_custom_call" | custom-call | flops 2147483648 | bytes 9437184 | tf_op jit(solution)/shard_map/pallas_call | solution.py:117
  158.3 0.0 collective-permute-done.12.refs_8_
  158.3 6.3 %shard_map.87 = bf16[4,512,512]{2,1,0:T(8,128)(2,1)S(1)} custom-call(s32[4]{0:T(128)S(1)} %and_select_fusion.4.order, s32[8]{0:T(128)S(1)} %fusion.7.places, bf16[128,1024]{1,0:T(8,128)(2,1)S(1)} %constant_dynamic-update-slice_fusion.refs_0_, bf16[128,1024]{1,0:T(8,128)(2,1)S(1)} %collective-permute-done.2.refs_1_, ...), custom_call_target="tpu_custom_call" | custom-call | flops 2147483648 | bytes 9437184 | tf_op jit(solution)/shard_map/pallas_call | solution.py:117
  164.7 35.5 %all_to_all.17 = bf16[16,128,512]{2,1,0:T(8,128)(2,1)S(1)} all-to-all(bf16[16,128,512]{2,1,0:T(8,128)(2,1)S(1)} %bitcast.36), channel_id=1, replica_groups=mesh['x'=4,'z'=16,'y'=4,'c'=2] {'x','y'}, dimensions={0} | all-to-all | bytes 4194304 | tf_op jit(solution)/shard_map/all_to_all | solution.py:178
  200.2 0.5 reduce_sum.52
  200.7 6.7 %collective-permute-start.13 = (bf16[4,2,64,512]{3,2,0,1:T(8,128)(2,1)S(1)}, bf16[4,2,64,512]{3,2,0,1:T(8,128)(2,1)S(1)}, u32[]{:S(2)}, u32[]{:S(2)}) collective-permute-start(bf16[4,2,64,512]{3,2,0,1:T(8,128)(2,1)S(1)} %copy.14), channel_id=1, source_target_pairs={{1,0},{0,1},{3,2},{2,3},{5,4},{4,5},{7,6},{6,7},{9,8},{8,9},{11,10... | collective-permute-start | bytes 1572872 | tf_op jit(solution)/shard_map/ppermute | solution.py:27
  207.5 1.5 collective-permute-done.13
  209.0 0.1 fusion.3
  209.1 1.0 copy.17
  (13 shorter events, 0.2 us)
Async XLA Ops:
  0.6 82.5 %copy-start = (bf16[512,1024]{1,0:T(8,128)(2,1)S(1)}, bf16[512,1024]{1,0:T(8,128)(2,1)}, u32[]{:S(2)}) copy-start(bf16[512,1024]{1,0:T(8,128)(2,1)} %refs_0_.1) | copy-start | bytes 3145732
  0.6 82.5 %collective-permute-start.9 = (bf16[512,1024]{1,0:T(8,128)(2,1)}, bf16[512,1024]{1,0:T(8,128)(2,1)S(1)}, u32[]{:S(2)}, u32[]{:S(2)}) collective-permute-start(bf16[512,1024]{1,0:T(8,128)(2,1)} %refs_0_.1), channel_id=1, source_target_pairs={{128,0},{129,1},{130,2},{131,3},{132,4},{133,5},{134,6},{135,7},{1... | collective-permute-start | bytes 3145736 | tf_op jit(solution)/shard_map/ppermute | solution.py:27
  6.0 77.2 %collective-permute-start.10 = (bf16[512,1024]{1,0:T(8,128)(2,1)}, bf16[512,1024]{1,0:T(8,128)(2,1)S(1)}, u32[]{:S(2)}, u32[]{:S(2)}) collective-permute-start(bf16[512,1024]{1,0:T(8,128)(2,1)} %refs_0_.1), channel_id=1, source_target_pairs={{384,0},{385,1},{386,2},{387,3},{388,4},{389,5},{390,6},{391,7},{3... | collective-permute-start | bytes 3145736 | tf_op jit(solution)/shard_map/ppermute | solution.py:27
  7.9 75.2 %collective-permute-start.11 = (bf16[512,1024]{1,0:T(8,128)(2,1)}, bf16[512,1024]{1,0:T(8,128)(2,1)}, u32[]{:S(2)}, u32[]{:S(2)}) collective-permute-start(bf16[512,1024]{1,0:T(8,128)(2,1)} %refs_0_.1), channel_id=1, source_target_pairs={{256,0},{257,1},{258,2},{259,3},{260,4},{261,5},{262,6},{263,7},{2... | collective-permute-start | bytes 3145736 | tf_op jit(solution)/shard_map/ppermute | solution.py:27
  83.1 3.7 %copy-start.1 = (f32[1024]{0:T(1024)}, f32[1024]{0:T(1024)S(1)}, u32[]{:S(2)}) copy-start(f32[1024]{0:T(1024)S(1)} %get-tuple-element.16) | copy-start | bytes 12292
  83.2 9.8 %copy-start.2 = (bf16[1024,64]{0,1:T(8,128)(2,1)S(1)}, bf16[1024,64]{0,1:T(8,128)(2,1)}, u32[]{:S(2)}) copy-start(bf16[1024,64]{0,1:T(8,128)(2,1)} %param.10) | copy-start | bytes 393220
  83.2 62.2 %copy-start.3 = (s32[4]{0:T(128)S(1)}, s32[4]{0:T(128)}, u32[]{:S(2)}) copy-start(s32[4]{0:T(128)} %constant.102.clone) | copy-start | bytes 52
  86.8 71.5 %collective-permute-start.12 = (bf16[4,512,1024]{2,1,0:T(8,128)(2,1)}, bf16[4,512,1024]{2,1,0:T(8,128)(2,1)}, u32[]{:S(2)}, u32[]{:S(2)}) collective-permute-start(bf16[4,512,1024]{2,1,0:T(8,128)(2,1)} %shard_map.85.refs_8_), channel_id=1, source_target_pairs={{1,0},{0,1},{3,2},{2,3},{5,4},{4,5},{7,6},{6,7},{9,8},{8,9},{11,10... | collective-permute-start | bytes 12582920 | tf_op jit(solution)/shard_map/ppermute | solution.py:27
  93.0 6.7 %collective-permute-start = (bf16[64,1024]{1,0:T(8,128)(2,1)S(1)}, bf16[64,1024]{1,0:T(8,128)(2,1)S(1)}, u32[]{:S(2)}, u32[]{:S(2)}) collective-permute-start(bf16[64,1024]{1,0:T(8,128)(2,1)S(1)} %bitcast.43), channel_id=1, source_target_pairs={{0,0},{129,1},{2,2},{131,3},{4,4},{133,5},{6,6},{135,7},{128,8},{2... | collective-permute-start | bytes 393224 | tf_op jit(solution)/shard_map/ppermute | solution.py:27
  97.0 6.3 %collective-permute-start.1 = (bf16[64,1024]{1,0:T(8,128)(2,1)S(1)}, bf16[64,1024]{1,0:T(8,128)(2,1)S(1)}, u32[]{:S(2)}, u32[]{:S(2)}) collective-permute-start(bf16[64,1024]{1,0:T(8,128)(2,1)S(1)} %bitcast.44), channel_id=1, source_target_pairs={{1,0},{128,1},{3,2},{130,3},{5,4},{132,5},{7,6},{134,7},{129,8},{2... | collective-permute-start | bytes 393224 | tf_op jit(solution)/shard_map/ppermute | solution.py:27
  103.3 15.7 %collective-permute-start.2 = (bf16[128,1024]{1,0:T(8,128)(2,1)S(1)}, bf16[128,1024]{1,0:T(8,128)(2,1)S(1)}, u32[]{:S(2)}, u32[]{:S(2)}) collective-permute-start(bf16[128,1024]{1,0:T(8,128)(2,1)S(1)} %constant_dynamic-update-slice_fusion.refs_0_), channel_id=1, source_target_pairs={{120,0},{9,1},{122,2},{11,3},{124,4},{13,5},{126,6},{15,7},{0,8},{... | collective-permute-start | bytes 786440 | tf_op jit(solution)/shard_map/ppermute | solution.py:27
  109.9 16.3 %collective-permute-start.3 = (bf16[128,1024]{1,0:T(8,128)(2,1)S(1)}, bf16[128,1024]{1,0:T(8,128)(2,1)S(1)}, u32[]{:S(2)}, u32[]{:S(2)}) collective-permute-start(bf16[128,1024]{1,0:T(8,128)(2,1)S(1)} %constant_dynamic-update-slice_fusion.refs_0_), channel_id=1, source_target_pairs={{112,0},{17,1},{114,2},{19,3},{116,4},{21,5},{118,6},{23,7},{120,8... | collective-permute-start | bytes 786440 | tf_op jit(solution)/shard_map/ppermute | solution.py:27
  119.0 11.4 %collective-permute-start.4 = (bf16[128,1024]{1,0:T(8,128)(2,1)S(1)}, bf16[128,1024]{1,0:T(8,128)(2,1)S(1)}, u32[]{:S(2)}, u32[]{:S(2)}) collective-permute-start(bf16[128,1024]{1,0:T(8,128)(2,1)S(1)} %collective-permute-done.2.refs_1_), channel_id=1, source_target_pairs={{112,0},{17,1},{114,2},{19,3},{116,4},{21,5},{118,6},{23,7},{120,8... | collective-permute-start | bytes 786440 | tf_op jit(solution)/shard_map/ppermute | solution.py:27
  126.1 11.3 %collective-permute-start.5 = (bf16[128,1024]{1,0:T(8,128)(2,1)S(1)}, bf16[128,1024]{1,0:T(8,128)(2,1)S(1)}, u32[]{:S(2)}, u32[]{:S(2)}) collective-permute-start(bf16[128,1024]{1,0:T(8,128)(2,1)S(1)} %collective-permute-done.3.refs_2_), channel_id=1, source_target_pairs={{112,0},{17,1},{114,2},{19,3},{116,4},{21,5},{118,6},{23,7},{120,8... | collective-permute-start | bytes 786440 | tf_op jit(solution)/shard_map/ppermute | solution.py:27
  130.4 11.9 %collective-permute-start.6 = (bf16[128,1024]{1,0:T(8,128)(2,1)S(1)}, bf16[128,1024]{1,0:T(8,128)(2,1)S(1)}, u32[]{:S(2)}, u32[]{:S(2)}) collective-permute-start(bf16[128,1024]{1,0:T(8,128)(2,1)S(1)} %collective-permute-done.4.refs_3_), channel_id=1, source_target_pairs={{112,0},{17,1},{114,2},{19,3},{116,4},{21,5},{118,6},{23,7},{120,8... | collective-permute-start | bytes 786440 | tf_op jit(solution)/shard_map/ppermute | solution.py:27
  137.4 11.9 %collective-permute-start.7 = (bf16[128,1024]{1,0:T(8,128)(2,1)S(1)}, bf16[128,1024]{1,0:T(8,128)(2,1)S(1)}, u32[]{:S(2)}, u32[]{:S(2)}) collective-permute-start(bf16[128,1024]{1,0:T(8,128)(2,1)S(1)} %collective-permute-done.5.refs_4_), channel_id=1, source_target_pairs={{112,0},{17,1},{114,2},{19,3},{116,4},{21,5},{118,6},{23,7},{120,8... | collective-permute-start | bytes 786440 | tf_op jit(solution)/shard_map/ppermute | solution.py:27
  142.3 9.7 %collective-permute-start.8 = (bf16[128,1024]{1,0:T(8,128)(2,1)S(1)}, bf16[128,1024]{1,0:T(8,128)(2,1)S(1)}, u32[]{:S(2)}, u32[]{:S(2)}) collective-permute-start(bf16[128,1024]{1,0:T(8,128)(2,1)S(1)} %collective-permute-done.6.refs_5_), channel_id=1, source_target_pairs={{112,0},{17,1},{114,2},{19,3},{116,4},{21,5},{118,6},{23,7},{120,8... | collective-permute-start | bytes 786440 | tf_op jit(solution)/shard_map/ppermute | solution.py:27
  200.7 8.2 %collective-permute-start.13 = (bf16[4,2,64,512]{3,2,0,1:T(8,128)(2,1)S(1)}, bf16[4,2,64,512]{3,2,0,1:T(8,128)(2,1)S(1)}, u32[]{:S(2)}, u32[]{:S(2)}) collective-permute-start(bf16[4,2,64,512]{3,2,0,1:T(8,128)(2,1)S(1)} %copy.14), channel_id=1, source_target_pairs={{1,0},{0,1},{3,2},{2,3},{5,4},{4,5},{7,6},{6,7},{9,8},{8,9},{11,10... | collective-permute-start | bytes 1572872 | tf_op jit(solution)/shard_map/ppermute | solution.py:27

commit v2 on v0

--- a/solution.py
+++ b/solution.py
@@ -15,7 +15,7 @@
 AXES = tuple(SIZES)
 SHAPE = tuple(SIZES.values())
 
-BLOCKS = (0, 1, 3, 2)
+BLOCKS = ((0, 1, 3, 2), (0, 3, 1, 2))
 
 
 def fetch(value, source):
@@ -27,8 +27,8 @@
     return lax.ppermute(value, AXES, pairs)
 
 
-def along_x(value, by):
-    return fetch(value, lambda x, z, y, c: (x + by, z, y, c))
+def along_x(value, k):
+    return fetch(value, lambda x, z, y, c: (x + BLOCKS[c][k], z, y, c))
 
 
 def holder(x, q):
@@ -58,7 +58,7 @@
 
 def normal(blocks, mean, factor):
     rows, depth = blocks[0].shape
-    tile = rows // 4
+    tile = rows // 2
     line = pl.BlockSpec((1, depth), lambda k: (0, 0))
     return pl.pallas_call(
         normal_kernel,
@@ -66,7 +66,7 @@
         grid=(rows // tile,),
         in_specs=[line, line] + [pl.BlockSpec((tile, depth), lambda k: (k, 0))] * 4,
         out_specs=pl.BlockSpec((4, tile, depth), lambda k: (0, k, 0)),
-        compiler_params=pltpu.CompilerParams(vmem_limit_bytes=12 * 1024 * 1024),
+        compiler_params=pltpu.CompilerParams(vmem_limit_bytes=24 * 1024 * 1024),
         cost_estimate=pl.CostEstimate(
             flops=20 * rows * depth, bytes_accessed=16 * rows * depth, transcendentals=0
         ),
@@ -104,22 +104,30 @@
     )
     if before:
         total = total + before[0][0].astype(jnp.float32)
-    out[0] = total.astype(out.dtype)
+    total = total.astype(out.dtype)
+    if before:
+        out[:, 0] = total.reshape(out.shape[0], *out.shape[2:])
+    else:
+        out[0] = total
 
 
 def product(side, order, places, slots, value, *before):
     _, rows, depth = value.shape
     columns = 4 * slots[0].shape[0]
-    to = (lambda k, order, *_: (order[k], 0, 0)) if before else (lambda k, *_: (k, 0, 0))
+    turned = lambda k, *_: (k + jnp.where(k == 1, 1, 0) - jnp.where(k == 2, 1, 0), 0, 0)
+    shape, block, to = (4, columns, rows), (1, columns, rows), lambda k, *_: (k, 0, 0)
+    if before:
+        shape, block = (4, 4, columns // 4, rows), (4, 1, columns // 4, rows)
+        to = lambda k, order, places: (0, order[k], 0, 0)
     return pl.pallas_call(
         functools.partial(product_kernel, side),
-        out_shape=jax.ShapeDtypeStruct((4, columns, rows), jnp.bfloat16),
+        out_shape=jax.ShapeDtypeStruct(shape, jnp.bfloat16),
         grid_spec=pltpu.PrefetchScalarGridSpec(
             num_scalar_prefetch=2,
             grid=(4,),
             in_specs=[pl.BlockSpec(memory_space=pl.ANY)] * 9
-            + [pl.BlockSpec((1, columns, rows), lambda k, *_: (k, 0, 0))] * len(before),
-            out_specs=pl.BlockSpec((1, columns, rows), to),
+            + [pl.BlockSpec((1, columns, rows), turned)] * len(before),
+            out_specs=pl.BlockSpec(block, to),
             scratch_shapes=[
                 pltpu.VMEM((columns, depth), jnp.bfloat16),
                 pltpu.VMEM(value.shape, jnp.bfloat16),
@@ -150,8 +158,8 @@
         )
     ]
     slots.append(along_z(slots[0], 1))
-    for k in range(2, 8):
-        slots.append(along_z(slots[k - 2], 2))
+    for k, start in ((2, 0), (3, 1), (4, 2), (5, 3), (6, 4), (7, 5)):
+        slots.append(along_z(slots[start], k - start))
 
     off = observations.astype(jnp.float32) - prior_mean
     sums = jnp.stack([jnp.sum(off, axis=0), jnp.sum(off * off, axis=0)])
@@ -163,17 +171,18 @@
     run_var = (prior_var * count + (sums[1] - sums[0] * sums[0] / total)) / total
     scale = 1.0 / jnp.sqrt(run_var + 1e-05)
 
-    blocks = [along_x(observations, by) if by else observations for by in BLOCKS]
+    blocks = [observations, along_x(observations, 1), along_x(observations, 2)]
+    blocks.append(along_x(blocks[1], 1))
     q = jnp.where(c == 0, z - jnp.arange(8), z + 1 + jnp.arange(8)) % 16
     places = (2 * (q % 4) + (q // 4) % 2).astype(jnp.int32)
-    order = ((x + jnp.array(BLOCKS)) % 4).astype(jnp.int32)
+    order = ((x + jnp.array(BLOCKS)[1 - c]) % 4).astype(jnp.int32)
     value = normal(blocks, run_mean, scale)
     part = product(0, order, places, slots, value)
     value = across(value)
     part = product(1, order, places, slots, value, part)
 
-    part = lax.all_to_all(part.reshape(16, -1, rows), ("x", "y"), 0, 0)
-    summed = part.reshape(4, 4, 2, -1, rows).astype(jnp.float32).sum(axis=1)
+    part = lax.all_to_all(part.reshape(16, -1, rows), ("y", "x"), 0, 0)
+    summed = part.reshape(4, 4, 2, -1, rows).astype(jnp.float32).sum(axis=0)
     summed = summed.astype(jnp.bfloat16)
     other = across(summed)
     sides = []

time: 212 us -> 202 us (0.953)
  the two profiles are of different devices: /device:TPU:1 before, /device:TPU:33 now
where the time goes in v2:
time: 202 us; the launch traced here: 201 us
  blocking collectives  73.6 us (36%)
  starting transfers between devices  54.2 us (27%)
  waiting for transfers between devices  51 us (25%)
  Pallas kernels  16.4 us (8%)
  other arithmetic  3.53 us (2%)
    ppermute x14, starting transfers between devices, fetch(): return lax.ppermute(value, AXES, pairs)  54.2 us
    ppermute x14, waiting for transfers between devices, fetch(): return lax.ppermute(value, AXES, pairs)  51 us
    all_to_all x2, blocking collectives, sum_over(): copies = lax.all_to_all(copies, axis, 0, 0)  39.7 us
    all_to_all x1, blocking collectives, step(): part = lax.all_to_all(part.reshape(16, -1, rows), ('y', 'x'), 0, 0)  33.9 us
    pallas_call x2, Pallas kernels, product(): pl.pallas_call(functools.partial(product_kernel, side), out_shape=jax.Sha...  12.8 us
  transfers between devices with their start and end apart: 14, of which 11 were waited for; matrix products, arithmetic and copies ran while one was open for 2% of the time, Pallas kernels for 3%

profile of v2, /device:TPU:33, one launch (start us, length us, event | category | flops | bytes accessed | tf_op | source)
XLA Modules:
  0.0 200.9 jit_solution(6459538228332935099)
XLA Ops:
  0.6 0.0 copy-start
  0.6 3.3 %collective-permute-start.9 = (bf16[512,1024]{1,0:T(8,128)(2,1)}, bf16[512,1024]{1,0:T(8,128)(2,1)S(1)}, u32[]{:S(2)}, u32[]{:S(2)}) collective-permute-start(bf16[512,1024]{1,0:T(8,128)(2,1)} %refs_0_.1), channel_id=1, source_target_pairs={{128,0},{385,1},{130,2},{387,3},{132,4},{389,5},{134,6},{391,7},{1... | collective-permute-start | bytes 3145736 | tf_op jit(solution)/shard_map/ppermute | solution.py:27
  3.9 3.4 %collective-permute-start.10 = (bf16[512,1024]{1,0:T(8,128)(2,1)}, bf16[512,1024]{1,0:T(8,128)(2,1)S(1)}, u32[]{:S(2)}, u32[]{:S(2)}) collective-permute-start(bf16[512,1024]{1,0:T(8,128)(2,1)} %refs_0_.1), channel_id=1, source_target_pairs={{384,0},{129,1},{386,2},{131,3},{388,4},{133,5},{390,6},{135,7},{3... | collective-permute-start | bytes 3145736 | tf_op jit(solution)/shard_map/ppermute | solution.py:27
  7.3 16.2 %collective-permute-done.9.refs_1_ = bf16[512,1024]{1,0:T(8,128)(2,1)S(1)} collective-permute-done((bf16[512,1024]{1,0:T(8,128)(2,1)}, bf16[512,1024]{1,0:T(8,128)(2,1)S(1)}, u32[]{:S(2)}, u32[]{:S(2)}) %collective-permute-start.9) | collective-permute-done | bytes 1048608 | tf_op jit(solution)/shard_map/ppermute | solution.py:27
  23.5 3.4 %collective-permute-start.11 = (bf16[512,1024]{1,0:T(8,128)(2,1)S(1)}, bf16[512,1024]{1,0:T(8,128)(2,1)}, u32[]{:S(2)}, u32[]{:S(2)}) collective-permute-start(bf16[512,1024]{1,0:T(8,128)(2,1)S(1)} %collective-permute-done.9.refs_1_), channel_id=1, source_target_pairs={{128,0},{385,1},{130,2},{387,3},{132,4},{389,5},{134,6},{391,7},{1... | collective-permute-start | bytes 3145736 | tf_op jit(solution)/shard_map/ppermute | solution.py:27
  26.8 1.6 fusion
  28.5 13.6 %all_to_all.15 = f32[4,16,128]{2,1,0:T(8,128)S(1)} all-to-all(f32[4,16,128]{2,1,0:T(8,128)S(1)} %broadcast_in_dim.21), channel_id=1, replica_groups=mesh['x'=4,'z'=16,'y'=4,'c'=2] {'x'}, dimensions={0} | all-to-all | bytes 65536 | tf_op jit(solution)/shard_map/all_to_all | solution.py:49
  42.1 26.1 %all_to_all.16 = f32[16,16,128]{2,1,0:T(8,128)S(1)} all-to-all(f32[16,16,128]{2,1,0:T(8,128)S(1)} %broadcast_in_dim.22), channel_id=1, replica_groups=mesh['x'=4,'z'=16,'y'=4,'c'=2] {'z'}, dimensions={0} | all-to-all | bytes 262144 | tf_op jit(solution)/shard_map/all_to_all | solution.py:49
  68.2 1.3 add_rsqrt_fusion
  69.6 0.0 copy-start.1
  69.6 0.0 collective-permute-done.10.refs_2_
  69.6 0.0 collective-permute-done.11.refs_3_
  69.6 0.0 copy-done
  69.6 0.0 copy-start.3
  69.6 0.0 copy-start.2
  69.6 3.7 %shard_map.85.refs_8_ = bf16[4,512,1024]{2,1,0:T(8,128)(2,1)} custom-call(f32[1,1024]{1,0:T(1,128)S(1)} %bitcast.39, f32[1,1024]{1,0:T(1,128)S(1)} %bitcast.40, bf16[512,1024]{1,0:T(8,128)(2,1)S(1)} %copy-done, bf16[512,1024]{1,0:T(8,128)(2,1)S(1)} %collective-permute-done.9.refs_1_, bf16[512,1024]{1,0:T(8,128)(2,1)S(1)} %collective-permute-done.10.refs_2_, ...), custom_call_target="tpu_custom_call" | custom-call | flops 10485760 | bytes 8388608 | tf_op jit(solution)/shard_map/pallas_call | solution.py:63
  73.3 0.0 copy-done.1
  73.3 8.2 %collective-permute-start.12 = (bf16[4,512,1024]{2,1,0:T(8,128)(2,1)}, bf16[4,512,1024]{2,1,0:T(8,128)(2,1)}, u32[]{:S(2)}, u32[]{:S(2)}) collective-permute-start(bf16[4,512,1024]{2,1,0:T(8,128)(2,1)} %shard_map.85.refs_8_), channel_id=1, source_target_pairs={{1,0},{0,1},{3,2},{2,3},{5,4},{4,5},{7,6},{6,7},{9,8},{8,9},{11,10... | collective-permute-start | bytes 12582920 | tf_op jit(solution)/shard_map/ppermute | solution.py:27
  81.5 0.0 copy-done.3
  81.5 5.2 %collective-permute-start = (bf16[64,1024]{1,0:T(8,128)(2,1)S(1)}, bf16[64,1024]{1,0:T(8,128)(2,1)S(1)}, u32[]{:S(2)}, u32[]{:S(2)}) collective-permute-start(bf16[64,1024]{1,0:T(8,128)(2,1)S(1)} %bitcast.45), channel_id=1, source_target_pairs={{0,0},{129,1},{2,2},{131,3},{4,4},{133,5},{6,6},{135,7},{128,8},{2... | collective-permute-start | bytes 393224 | tf_op jit(solution)/shard_map/ppermute | solution.py:27
  86.7 1.9 collective-permute-start.1
  88.6 12.4 %collective-permute-done = bf16[64,1024]{1,0:T(8,128)(2,1)S(1)} collective-permute-done((bf16[64,1024]{1,0:T(8,128)(2,1)S(1)}, bf16[64,1024]{1,0:T(8,128)(2,1)S(1)}, u32[]{:S(2)}, u32[]{:S(2)}) %collective-permute-start) | collective-permute-done | bytes 131104 | tf_op jit(solution)/shard_map/ppermute | solution.py:27
  101.1 1.6 collective-permute-done.1
  102.7 1.9 collective-permute-start.2
  104.6 1.9 collective-permute-start.3
  106.6 3.3 %collective-permute-done.2.refs_1_ = bf16[128,1024]{1,0:T(8,128)(2,1)S(1)} collective-permute-done((bf16[128,1024]{1,0:T(8,128)(2,1)S(1)}, bf16[128,1024]{1,0:T(8,128)(2,1)S(1)}, u32[]{:S(2)}, u32[]{:S(2)}) %collective-permute-start.2) | collective-permute-done | bytes 262176 | tf_op jit(solution)/shard_map/ppermute | solution.py:27
  109.8 1.9 collective-permute-start.4
  111.7 1.3 collective-permute-done.3.refs_2_
  113.0 3.8 %collective-permute-start.5 = (bf16[128,1024]{1,0:T(8,128)(2,1)S(1)}, bf16[128,1024]{1,0:T(8,128)(2,1)S(1)}, u32[]{:S(2)}, u32[]{:S(2)}) collective-permute-start(bf16[128,1024]{1,0:T(8,128)(2,1)S(1)} %collective-permute-done.3.refs_2_), channel_id=1, source_target_pairs={{112,0},{17,1},{114,2},{19,3},{116,4},{21,5},{118,6},{23,7},{120,8... | collective-permute-start | bytes 786440 | tf_op jit(solution)/shard_map/ppermute | solution.py:27
  116.8 5.0 %collective-permute-done.4.refs_3_ = bf16[128,1024]{1,0:T(8,128)(2,1)S(1)} collective-permute-done((bf16[128,1024]{1,0:T(8,128)(2,1)S(1)}, bf16[128,1024]{1,0:T(8,128)(2,1)S(1)}, u32[]{:S(2)}, u32[]{:S(2)}) %collective-permute-start.4) | collective-permute-done | bytes 262176 | tf_op jit(solution)/shard_map/ppermute | solution.py:27
  121.8 4.5 %collective-permute-start.6 = (bf16[128,1024]{1,0:T(8,128)(2,1)S(1)}, bf16[128,1024]{1,0:T(8,128)(2,1)S(1)}, u32[]{:S(2)}, u32[]{:S(2)}) collective-permute-start(bf16[128,1024]{1,0:T(8,128)(2,1)S(1)} %collective-permute-done.4.refs_3_), channel_id=1, source_target_pairs={{112,0},{17,1},{114,2},{19,3},{116,4},{21,5},{118,6},{23,7},{120,8... | collective-permute-start | bytes 786440 | tf_op jit(solution)/shard_map/ppermute | solution.py:27
  126.3 1.5 collective-permute-done.5.refs_4_
  127.8 4.7 %collective-permute-start.7 = (bf16[128,1024]{1,0:T(8,128)(2,1)S(1)}, bf16[128,1024]{1,0:T(8,128)(2,1)S(1)}, u32[]{:S(2)}, u32[]{:S(2)}) collective-permute-start(bf16[128,1024]{1,0:T(8,128)(2,1)S(1)} %collective-permute-done.5.refs_4_), channel_id=1, source_target_pairs={{112,0},{17,1},{114,2},{19,3},{116,4},{21,5},{118,6},{23,7},{120,8... | collective-permute-start | bytes 786440 | tf_op jit(solution)/shard_map/ppermute | solution.py:27
  132.4 0.6 collective-permute-done.6.refs_5_
  133.1 4.7 %collective-permute-start.8 = (bf16[128,1024]{1,0:T(8,128)(2,1)S(1)}, bf16[128,1024]{1,0:T(8,128)(2,1)S(1)}, u32[]{:S(2)}, u32[]{:S(2)}) collective-permute-start(bf16[128,1024]{1,0:T(8,128)(2,1)S(1)} %collective-permute-done.6.refs_5_), channel_id=1, source_target_pairs={{112,0},{17,1},{114,2},{19,3},{116,4},{21,5},{118,6},{23,7},{120,8... | collective-permute-start | bytes 786440 | tf_op jit(solution)/shard_map/ppermute | solution.py:27
  137.8 0.0 copy-done.2
  137.9 4.9 %collective-permute-done.7.refs_6_ = bf16[128,1024]{1,0:T(8,128)(2,1)S(1)} collective-permute-done((bf16[128,1024]{1,0:T(8,128)(2,1)S(1)}, bf16[128,1024]{1,0:T(8,128)(2,1)S(1)}, u32[]{:S(2)}, u32[]{:S(2)}) %collective-permute-start.7) | collective-permute-done | bytes 262176 | tf_op jit(solution)/shard_map/ppermute | solution.py:27
  142.7 2.8 %collective-permute-done.8.refs_7_ = bf16[128,1024]{1,0:T(8,128)(2,1)S(1)} collective-permute-done((bf16[128,1024]{1,0:T(8,128)(2,1)S(1)}, bf16[128,1024]{1,0:T(8,128)(2,1)S(1)}, u32[]{:S(2)}, u32[]{:S(2)}) %collective-permute-start.8) | collective-permute-done | bytes 262176 | tf_op jit(solution)/shard_map/ppermute | solution.py:27
  145.5 6.3 %shard_map.86.refs_9_ = bf16[4,512,512]{2,1,0:T(8,128)(2,1)S(1)} custom-call(s32[4]{0:T(128)S(1)} %and_select_fusion.4.order, s32[8]{0:T(128)S(1)} %fusion.7.places, bf16[128,1024]{1,0:T(8,128)(2,1)S(1)} %constant_dynamic-update-slice_fusion.refs_0_, bf16[128,1024]{1,0:T(8,128)(2,1)S(1)} %collective-permute-done.2.refs_1_, ...), custom_call_target="tpu_custom_call" | custom-call | flops 2147483648 | bytes 9437184 | tf_op jit(solution)/shard_map/pallas_call | solution.py:122
  151.8 0.0 collective-permute-done.12.refs_8_
  151.8 6.5 %shard_map.87 = bf16[4,4,128,512]{3,2,1,0:T(8,128)(2,1)S(1)} custom-call(s32[4]{0:T(128)S(1)} %and_select_fusion.4.order, s32[8]{0:T(128)S(1)} %fusion.7.places, bf16[128,1024]{1,0:T(8,128)(2,1)S(1)} %constant_dynamic-update-slice_fusion.refs_0_, bf16[128,1024]{1,0:T(8,128)(2,1)S(1)} %collective-permute-done.2.refs_1_, ...), custom_call_target="tpu_custom_call" | custom-call | flops 2147483648 | bytes 9437184 | tf_op jit(solution)/shard_map/pallas_call | solution.py:122
  158.3 33.9 %all_to_all.17 = bf16[16,128,512]{2,1,0:T(8,128)(2,1)S(1)} all-to-all(bf16[16,128,512]{2,1,0:T(8,128)(2,1)S(1)} %bitcast.38), channel_id=1, replica_groups=mesh['x'=4,'z'=16,'y'=4,'c'=2] {'y','x'}, dimensions={0} | all-to-all | bytes 4194304 | tf_op jit(solution)/shard_map/all_to_all | solution.py:184
  192.2 0.4 reduce_sum.52
  192.7 5.5 %collective-permute-start.13 = (bf16[4,2,64,512]{3,2,0,1:T(8,128)(2,1)S(1)}, bf16[4,2,64,512]{3,2,0,1:T(8,128)(2,1)S(1)}, u32[]{:S(2)}, u32[]{:S(2)}) collective-permute-start(bf16[4,2,64,512]{3,2,0,1:T(8,128)(2,1)S(1)} %copy.14), channel_id=1, source_target_pairs={{1,0},{0,1},{3,2},{2,3},{5,4},{4,5},{7,6},{6,7},{9,8},{8,9},{11,10... | collective-permute-start | bytes 1572872 | tf_op jit(solution)/shard_map/ppermute | solution.py:27
  198.2 1.5 collective-permute-done.13
  199.7 0.1 fusion.3
  199.9 1.0 copy.17
  (13 shorter events, 0.2 us)
Async XLA Ops:
  0.6 69.0 %copy-start = (bf16[512,1024]{1,0:T(8,128)(2,1)S(1)}, bf16[512,1024]{1,0:T(8,128)(2,1)}, u32[]{:S(2)}) copy-start(bf16[512,1024]{1,0:T(8,128)(2,1)} %refs_0_.1) | copy-start | bytes 3145732
  0.6 22.8 %collective-permute-start.9 = (bf16[512,1024]{1,0:T(8,128)(2,1)}, bf16[512,1024]{1,0:T(8,128)(2,1)S(1)}, u32[]{:S(2)}, u32[]{:S(2)}) collective-permute-start(bf16[512,1024]{1,0:T(8,128)(2,1)} %refs_0_.1), channel_id=1, source_target_pairs={{128,0},{385,1},{130,2},{387,3},{132,4},{389,5},{134,6},{391,7},{1... | collective-permute-start | bytes 3145736 | tf_op jit(solution)/shard_map/ppermute | solution.py:27
  3.9 65.7 %collective-permute-start.10 = (bf16[512,1024]{1,0:T(8,128)(2,1)}, bf16[512,1024]{1,0:T(8,128)(2,1)S(1)}, u32[]{:S(2)}, u32[]{:S(2)}) collective-permute-start(bf16[512,1024]{1,0:T(8,128)(2,1)} %refs_0_.1), channel_id=1, source_target_pairs={{384,0},{129,1},{386,2},{131,3},{388,4},{133,5},{390,6},{135,7},{3... | collective-permute-start | bytes 3145736 | tf_op jit(solution)/shard_map/ppermute | solution.py:27
  23.5 46.1 %collective-permute-start.11 = (bf16[512,1024]{1,0:T(8,128)(2,1)S(1)}, bf16[512,1024]{1,0:T(8,128)(2,1)}, u32[]{:S(2)}, u32[]{:S(2)}) collective-permute-start(bf16[512,1024]{1,0:T(8,128)(2,1)S(1)} %collective-permute-done.9.refs_1_), channel_id=1, source_target_pairs={{128,0},{385,1},{130,2},{387,3},{132,4},{389,5},{134,6},{391,7},{1... | collective-permute-start | bytes 3145736 | tf_op jit(solution)/shard_map/ppermute | solution.py:27
  69.6 3.7 %copy-start.1 = (f32[1024]{0:T(1024)}, f32[1024]{0:T(1024)S(1)}, u32[]{:S(2)}) copy-start(f32[1024]{0:T(1024)S(1)} %get-tuple-element.16) | copy-start | bytes 12292
  69.6 11.9 %copy-start.3 = (bf16[1024,64]{0,1:T(8,128)(2,1)S(1)}, bf16[1024,64]{0,1:T(8,128)(2,1)}, u32[]{:S(2)}) copy-start(bf16[1024,64]{0,1:T(8,128)(2,1)} %param.10) | copy-start | bytes 393220
  69.6 68.2 %copy-start.2 = (s32[2,4]{1,0:T(2,128)S(1)}, s32[2,4]{1,0:T(2,128)}, u32[]{:S(2)}) copy-start(s32[2,4]{1,0:T(2,128)} %constant.103.clone) | copy-start | bytes 100
  73.3 78.6 %collective-permute-start.12 = (bf16[4,512,1024]{2,1,0:T(8,128)(2,1)}, bf16[4,512,1024]{2,1,0:T(8,128)(2,1)}, u32[]{:S(2)}, u32[]{:S(2)}) collective-permute-start(bf16[4,512,1024]{2,1,0:T(8,128)(2,1)} %shard_map.85.refs_8_), channel_id=1, source_target_pairs={{1,0},{0,1},{3,2},{2,3},{5,4},{4,5},{7,6},{6,7},{9,8},{8,9},{11,10... | collective-permute-start | bytes 12582920 | tf_op jit(solution)/shard_map/ppermute | solution.py:27
  81.5 19.6 %collective-permute-start = (bf16[64,1024]{1,0:T(8,128)(2,1)S(1)}, bf16[64,1024]{1,0:T(8,128)(2,1)S(1)}, u32[]{:S(2)}, u32[]{:S(2)}) collective-permute-start(bf16[64,1024]{1,0:T(8,128)(2,1)S(1)} %bitcast.45), channel_id=1, source_target_pairs={{0,0},{129,1},{2,2},{131,3},{4,4},{133,5},{6,6},{135,7},{128,8},{2... | collective-permute-start | bytes 393224 | tf_op jit(solution)/shard_map/ppermute | solution.py:27
  86.7 16.0 %collective-permute-start.1 = (bf16[64,1024]{1,0:T(8,128)(2,1)S(1)}, bf16[64,1024]{1,0:T(8,128)(2,1)S(1)}, u32[]{:S(2)}, u32[]{:S(2)}) collective-permute-start(bf16[64,1024]{1,0:T(8,128)(2,1)S(1)} %bitcast.46), channel_id=1, source_target_pairs={{1,0},{128,1},{3,2},{130,3},{5,4},{132,5},{7,6},{134,7},{129,8},{2... | collective-permute-start | bytes 393224 | tf_op jit(solution)/shard_map/ppermute | solution.py:27
  102.7 7.1 %collective-permute-start.2 = (bf16[128,1024]{1,0:T(8,128)(2,1)S(1)}, bf16[128,1024]{1,0:T(8,128)(2,1)S(1)}, u32[]{:S(2)}, u32[]{:S(2)}) collective-permute-start(bf16[128,1024]{1,0:T(8,128)(2,1)S(1)} %constant_dynamic-update-slice_fusion.refs_0_), channel_id=1, source_target_pairs={{120,0},{9,1},{122,2},{11,3},{124,4},{13,5},{126,6},{15,7},{0,8},{... | collective-permute-start | bytes 786440 | tf_op jit(solution)/shard_map/ppermute | solution.py:27
  104.6 8.4 %collective-permute-start.3 = (bf16[128,1024]{1,0:T(8,128)(2,1)S(1)}, bf16[128,1024]{1,0:T(8,128)(2,1)S(1)}, u32[]{:S(2)}, u32[]{:S(2)}) collective-permute-start(bf16[128,1024]{1,0:T(8,128)(2,1)S(1)} %constant_dynamic-update-slice_fusion.refs_0_), channel_id=1, source_target_pairs={{112,0},{17,1},{114,2},{19,3},{116,4},{21,5},{118,6},{23,7},{120,8... | collective-permute-start | bytes 786440 | tf_op jit(solution)/shard_map/ppermute | solution.py:27
  109.8 12.0 %collective-permute-start.4 = (bf16[128,1024]{1,0:T(8,128)(2,1)S(1)}, bf16[128,1024]{1,0:T(8,128)(2,1)S(1)}, u32[]{:S(2)}, u32[]{:S(2)}) collective-permute-start(bf16[128,1024]{1,0:T(8,128)(2,1)S(1)} %collective-permute-done.2.refs_1_), channel_id=1, source_target_pairs={{112,0},{17,1},{114,2},{19,3},{116,4},{21,5},{118,6},{23,7},{120,8... | collective-permute-start | bytes 786440 | tf_op jit(solution)/shard_map/ppermute | solution.py:27
  113.0 14.7 %collective-permute-start.5 = (bf16[128,1024]{1,0:T(8,128)(2,1)S(1)}, bf16[128,1024]{1,0:T(8,128)(2,1)S(1)}, u32[]{:S(2)}, u32[]{:S(2)}) collective-permute-start(bf16[128,1024]{1,0:T(8,128)(2,1)S(1)} %collective-permute-done.3.refs_2_), channel_id=1, source_target_pairs={{112,0},{17,1},{114,2},{19,3},{116,4},{21,5},{118,6},{23,7},{120,8... | collective-permute-start | bytes 786440 | tf_op jit(solution)/shard_map/ppermute | solution.py:27
  121.8 11.3 %collective-permute-start.6 = (bf16[128,1024]{1,0:T(8,128)(2,1)S(1)}, bf16[128,1024]{1,0:T(8,128)(2,1)S(1)}, u32[]{:S(2)}, u32[]{:S(2)}) collective-permute-start(bf16[128,1024]{1,0:T(8,128)(2,1)S(1)} %collective-permute-done.4.refs_3_), channel_id=1, source_target_pairs={{112,0},{17,1},{114,2},{19,3},{116,4},{21,5},{118,6},{23,7},{120,8... | collective-permute-start | bytes 786440 | tf_op jit(solution)/shard_map/ppermute | solution.py:27
  127.8 15.0 %collective-permute-start.7 = (bf16[128,1024]{1,0:T(8,128)(2,1)S(1)}, bf16[128,1024]{1,0:T(8,128)(2,1)S(1)}, u32[]{:S(2)}, u32[]{:S(2)}) collective-permute-start(bf16[128,1024]{1,0:T(8,128)(2,1)S(1)} %collective-permute-done.5.refs_4_), channel_id=1, source_target_pairs={{112,0},{17,1},{114,2},{19,3},{116,4},{21,5},{118,6},{23,7},{120,8... | collective-permute-start | bytes 786440 | tf_op jit(solution)/shard_map/ppermute | solution.py:27
  133.1 12.5 %collective-permute-start.8 = (bf16[128,1024]{1,0:T(8,128)(2,1)S(1)}, bf16[128,1024]{1,0:T(8,128)(2,1)S(1)}, u32[]{:S(2)}, u32[]{:S(2)}) collective-permute-start(bf16[128,1024]{1,0:T(8,128)(2,1)S(1)} %collective-permute-done.6.refs_5_), channel_id=1, source_target_pairs={{112,0},{17,1},{114,2},{19,3},{116,4},{21,5},{118,6},{23,7},{120,8... | collective-permute-start | bytes 786440 | tf_op jit(solution)/shard_map/ppermute | solution.py:27
  192.7 7.0 %collective-permute-start.13 = (bf16[4,2,64,512]{3,2,0,1:T(8,128)(2,1)S(1)}, bf16[4,2,64,512]{3,2,0,1:T(8,128)(2,1)S(1)}, u32[]{:S(2)}, u32[]{:S(2)}) collective-permute-start(bf16[4,2,64,512]{3,2,0,1:T(8,128)(2,1)S(1)} %copy.14), channel_id=1, source_target_pairs={{1,0},{0,1},{3,2},{2,3},{5,4},{4,5},{7,6},{6,7},{9,8},{8,9},{11,10... | collective-permute-start | bytes 1572872 | tf_op jit(solution)/shard_map/ppermute | solution.py:27
